TPU v7x, 32 devices: a whole 2x2x4 slice. The times are simulated.
32 devices in a mesh: pb: 4 (over x, core), pq: 8 (over z, y).
Axes of the slice: x: 2, y: 2, z: 4, core: 2. Of those that a mesh axis runs over, the one named last changes fastest.
Arguments:
- chol_vv: bfloat16 [176, 1792, 1792], P('pb', 'pq'), may hold values from -6 to 6
- chol_ov: bfloat16 [176, 256, 1792], P('pb', 'pq'), may hold values from -6 to 6
- chol_oo: bfloat16 [176, 256, 256], P('pb', 'pq'), may hold values from -6 to 6
- chol_vo: bfloat16 [176, 256, 1792], P('pb', None, 'pq'), may hold values from -6 to 6
- amplitudes: bfloat16 [256, 1792], P(None, 'pq'), may hold values from -0.125 to 0.125
Outputs:
- dressed: bfloat16 [176, 256, 1792], P('pb', 'pq')
- fock_ov: float32 [256, 1792], P('pq')
All inputs are finite; a program needn't handle non-finite values.
Results may differ from a plain program's by a relative error of at most 0.0081.
Values may be sent and summed in bfloat16 or wider, within the bound.
A program may use at most 128 MiB of HBM per device.

v0:
```python
import jax
import jax.numpy as jnp
from jax import lax
from jax.sharding import PartitionSpec as P


def per_device(chol_vv, chol_ov, chol_oo, chol_vo, amplitudes):
    batch = chol_vv.shape[0]
    occ_rows = chol_ov.shape[1]
    whole_amps = lax.all_gather(amplitudes, "pq", axis=1, tiled=True)
    lprime = (
        chol_oo.astype(jnp.float32)
        + jnp.einsum("qjb,ib->qji", chol_ov, whole_amps, preferred_element_type=jnp.float32)
    ).astype(jnp.bfloat16)
    direct = jnp.einsum("qab,ib->qia", chol_vv, whole_amps, preferred_element_type=jnp.float32)
    partial_sum = chol_vo.astype(jnp.float32) + direct
    occupied = jnp.einsum(
        "qji,ja->qia",
        lax.all_gather(lprime, "pq", axis=1, tiled=True),
        amplitudes,
        preferred_element_type=jnp.float32,
    )
    local_dressed = (partial_sum - occupied).astype(jnp.bfloat16)
    dressed = lax.all_to_all(local_dressed, "pq", split_axis=1, concat_axis=2, tiled=True)
    row_start = lax.axis_index("pq") * occ_rows
    own_amps = lax.dynamic_slice_in_dim(whole_amps, row_start, occ_rows, 0)
    local_coulomb = 2.0 * jnp.einsum(
        "qia,ia->q", dressed, own_amps, preferred_element_type=jnp.float32
    )
    coulomb = lax.psum(local_coulomb, "pq")
    local_fock = jnp.sum(coulomb[:, None, None] * dressed.astype(jnp.float32), axis=0)
    fock_ov = lax.psum(local_fock, "pb") / (batch * lax.axis_size("pb"))
    return (dressed, fock_ov)


def solution(mesh):
    in_specs = (
        P("pb", "pq", None),
        P("pb", "pq", None),
        P("pb", "pq", None),
        P("pb", None, "pq"),
        P(None, "pq"),
    )
    out_specs = (P("pb", "pq", None), P("pq", None))
    return jax.shard_map(
        per_device, mesh=mesh, in_specs=in_specs, out_specs=out_specs, check_vma=False
    )
```

profile of v0, /device:TPU:0, one launch (start us, length us, event | category | flops | bytes accessed | tf_op | source)
XLA Modules:
  0.0 394.0 jit_solution(11344486963419450905)
XLA Ops:
  7.2 0.0 all-gather.2.cloned.1.call-start
  7.2 34.5 %all_gather.6 = bf16[256,1792]{0,1:T(8,128)(2,1)S(1)} all-gather(bf16[256,224]{0,1:T(8,128)(2,1)} %param.9), channel_id=1, replica_groups=mesh['pb'=4,'pq'=8] {'pq'}, dimensions={1}, use_global_device_ids=true | all-gather | bytes 1032192 | tf_op jit(solution)/shard_map/all_gather | solution.py:10
  41.7 5.0 %add_convert_fusion = bf16[44,32,256]{2,1,0:T(8,128)(2,1)} fusion(bf16[44,32,256]{2,1,0:T(8,128)(2,1)} %param.7, bf16[44,32,1792]{2,1,0:T(8,128)(2,1)} %param.6, bf16[256,1792]{0,1:T(8,128)(2,1)S(1)} %all_gather.6), kind=kOutput, calls=%fused_computation.6 | convolution fusion | flops 1292926976 | bytes 7405568 | tf_op jit(solution)/shard_map/qjb,ib->qji/dot_general | solution.py:13
  46.6 0.0 all-gather.2.cloned.1.call-update
  46.7 19.8 %fusion.11 = f32[256,44,224]{0,2,1:T(8,128)} fusion(bf16[44,224,1792]{2,1,0:T(8,128)(2,1)} %param.5, bf16[256,1792]{0,1:T(8,128)(2,1)S(1)} %all_gather.6), kind=kOutput, calls=%fused_computation.10 | convolution fusion | flops 9042919424 | bytes 46333952 | tf_op jit(solution)/shard_map/qab,ib->qia/dot_general | solution.py:15
  66.4 73.5 %all-gather.2.cloned.1.call-done = bf16[44,256,256]{2,1,0:T(8,128)(2,1)} async-done(((bf16[44,32,256]{2,1,0:T(8,128)(2,1)}), bf16[44,256,256]{2,1,0:T(8,128)(2,1)}) %all-gather.2.cloned.1.call-update) | async-done | bytes 5767184 | tf_op jit(solution)/shard_map/all_gather | solution.py:19
  139.9 10.7 %fusion.1 = bf16[44,256,224]{1,2,0:T(8,128)(2,1)} fusion(f32[256,44,224]{0,2,1:T(8,128)} %fusion.11, bf16[44,256,224]{1,2,0:T(8,128)(2,1)} %param.8, bf16[44,256,256]{2,1,0:T(8,128)(2,1)} %all-gather.2.cloned.1.call-done, bf16[256,224]{0,1:T(8,128)(2,1)S(1)} %copy-done), kind=kOutput, calls=%fused_computation.3 | convolution fusion | flops 1301938176 | bytes 26066944 | tf_op jit(solution)/shard_map/qji,ja->qia/dot_general | solution.py:17
  150.6 8.8 %copy.14 = bf16[44,256,224]{2,0,1:T(8,128)(2,1)} copy(bf16[44,256,224]{1,2,0:T(8,128)(2,1)} %fusion.1) | data formatting | bytes 10092544 | tf_op jit(solution)/shard_map/convert_element_type | solution.py:23
  159.5 4.7 %all-to-all-start = ((bf16[44,256,224]{2,0,1:T(8,128)(2,1)}), bf16[44,256,224]{2,0,1:T(8,128)(2,1)}, u32[]{:S(2)}, u32[]{:S(2)}) async-start(bf16[44,256,224]{2,0,1:T(8,128)(2,1)} %copy.14), calls=%async_computation | async-start | bytes 12582912 | tf_op jit(solution)/shard_map/all_to_all | solution.py:24
  164.2 0.2 all-reduce.2.cloned.1.call-start
  164.5 0.2 dynamic-slice_bitcast_fusion
  164.7 0.3 copy.19
  165.0 136.1 %all-to-all-done = bf16[44,256,224]{2,0,1:T(8,128)(2,1)} async-done(((bf16[44,256,224]{2,0,1:T(8,128)(2,1)}), bf16[44,256,224]{2,0,1:T(8,128)(2,1)}, u32[]{:S(2)}, u32[]{:S(2)}) %all-to-all-start) | async-done | bytes 5046304 | tf_op jit(solution)/shard_map/all_to_all | solution.py:24
  301.1 8.6 %copy.16 = bf16[44,32,8,224]{3,2,1,0:T(8,128)(2,1)} copy(bf16[44,32,8,224]{3,0,1,2:T(8,128)(2,1)} %bitcast.5) | data formatting | bytes 10092544 | tf_op jit(solution)/shard_map/all_to_all | solution.py:24
  309.7 11.0 %all_to_all.16 = bf16[44,32,1792]{2,1,0:T(8,128)(2,1)} reshape(bf16[44,32,8,224]{3,2,1,0:T(8,128)(2,1)} %copy.16) | data formatting | bytes 10092544 | tf_op jit(solution)/shard_map/all_to_all | solution.py:24
  320.7 7.9 %fusion.7 = f32[44]{0:T(128)S(1)} fusion(bf16[32,1792,1]{1,2,0:T(2,128)(2,1)S(1)} %copy.19, bf16[44,32,1792]{2,1,0:T(8,128)(2,1)} %all_to_all.16), kind=kOutput, calls=%fused_computation.8 | convolution fusion | flops 5046316 | bytes 5161136 | tf_op jit(solution)/shard_map/qia,ia->q/dot_general | solution.py:27
  328.5 19.7 %psum.14 = f32[44]{0:T(128)S(1)} all-reduce(f32[44]{0:T(128)S(1)} %fusion.7), channel_id=1, replica_groups=mesh['pb'=4,'pq'=8] {'pq'}, use_global_device_ids=true, to_apply=%region_0.0 | all-reduce | flops 44 | bytes 352 | tf_op jit(solution)/shard_map/psum | solution.py:30
  348.2 4.8 %copy.15 = bf16[44,256,224]{2,1,0:T(8,128)(2,1)S(1)} copy(bf16[44,256,224]{2,0,1:T(8,128)(2,1)} %all-to-all-done) | data formatting | bytes 10092544 | tf_op jit(solution)/shard_map/all_to_all | solution.py:24
  353.0 1.9 multiply_reduce_fusion
  354.9 0.2 copy.17
  355.0 0.8 reduce_sum.12
  355.9 0.0 all-reduce.2.cloned.1.call-update
  355.9 29.6 %all-reduce.2.cloned.1.call-done = f32[32,1792]{1,0:T(8,128)} async-done(((f32[32,1792]{1,0:T(8,128)}), f32[32,1792]{1,0:T(8,128)}) %all-reduce.2.cloned.1.call-update) | async-done | bytes 229392 | tf_op jit(solution)/shard_map/psum | solution.py:32
  385.5 1.6 broadcast_multiply_fusion
  (2 shorter events, 0.0 us)
Async XLA Ops:
  7.2 132.8 %all-gather.2.cloned.1.call-start = ((), (), s32[]{:S(2)}) async-start(), calls=%async_computation.1 | async-start | bytes 6488064 | tf_op jit(solution)/shard_map/all_gather | solution.py:19
  46.6 93.3 %copy-start = (bf16[256,224]{0,1:T(8,128)(2,1)S(1)}, bf16[256,224]{0,1:T(8,128)(2,1)}, u32[]{:S(2)}) copy-start(bf16[256,224]{0,1:T(8,128)(2,1)} %param.9) | copy-start | bytes 344068
  159.5 141.6 %all-to-all-start = ((bf16[44,256,224]{2,0,1:T(8,128)(2,1)}), bf16[44,256,224]{2,0,1:T(8,128)(2,1)}, u32[]{:S(2)}, u32[]{:S(2)}) async-start(bf16[44,256,224]{2,0,1:T(8,128)(2,1)} %copy.14), calls=%async_computation | async-start | bytes 12582912 | tf_op jit(solution)/shard_map/all_to_all | solution.py:24
  164.2 221.2 %all-reduce.2.cloned.1.call-start = ((), (), s32[]{:S(2)}) async-start(), calls=%async_computation.2 | async-start | bytes 458752 | tf_op jit(solution)/shard_map/psum | solution.py:32
Sparse Core Ops, SparseCore 0:
  46.8 93.1 all-gather.1
  356.0 29.4 all-reduce.1
where the time goes:
time: 395 us; the launch traced here: 394 us
  waiting for transfers between devices  239 us (61%)
  blocking collectives  54.1 us (14%)
  matrix products  43.3 us (11%)
  local copies, waits for them, and re-layouts  34.7 us (9%)
  between operations  14.1 us (4%)
  starting transfers between devices  5.01 us (1%)
    all_to_all x1, waiting for transfers between devices, per_device(): lax.all_to_all(local_dressed, 'pq', split_axis=1, concat_axis=2, tiled=True)  136 us
    all_gather x1, waiting for transfers between devices, per_device(): lax.all_gather(lprime, 'pq', axis=1, tiled=True)  73.5 us
    all_gather x1, blocking collectives, per_device(): whole_amps = lax.all_gather(amplitudes, 'pq', axis=1, tiled=True)  34.5 us
    psum x1, waiting for transfers between devices, per_device(): fock_ov = lax.psum(local_fock, 'pb') / (batch * lax.axis_size('pb'))  29.6 us
    all_to_all x3, local copies, waits for them, and re-layouts, per_device(): lax.all_to_all(local_dressed, 'pq', split_axis=1, concat_axis=2, tiled=True)  24.4 us
    dot_general x1, matrix products, per_device(): jnp.einsum('qab,ib->qia', chol_vv, whole_amps, preferred_element_type=jnp...  19.8 us
    psum x1, blocking collectives, per_device(): coulomb = lax.psum(local_coulomb, 'pq')  19.7 us
    dot_general x1, matrix products, per_device(): jnp.einsum('qji,ja->qia', lax.all_gather(lprime, 'pq', axis=1, tiled=True...  10.7 us
  transfers between devices with their start and end apart: 3, of which 3 were waited for; matrix products, arithmetic and copies ran while one was open for 5% of the time, Pallas kernels for 0%

commit v1 on v0

--- a/solution.py
+++ b/solution.py
@@ -2,6 +2,11 @@
 import jax.numpy as jnp
 from jax import lax
 from jax.sharding import PartitionSpec as P
+
+
+def register_shelves_now(field_in, lane_axis):
+    z = jnp.sum(lax.all_gather(field_in, lane_axis), axis=0)
+    return z
 
 
 def per_device(chol_vv, chol_ov, chol_oo, chol_vo, amplitudes):
@@ -29,7 +34,7 @@
     )
     coulomb = lax.psum(local_coulomb, "pq")
     local_fock = jnp.sum(coulomb[:, None, None] * dressed.astype(jnp.float32), axis=0)
-    fock_ov = lax.psum(local_fock, "pb") / (batch * lax.axis_size("pb"))
+    fock_ov = register_shelves_now(local_fock, "pb") / (batch * lax.axis_size("pb"))
     return (dressed, fock_ov)
 
 

time: 395 us -> 373 us (0.944)
  waiting for transfers between devices: 239 us -> 210 us
  blocking collectives: 54.1 us -> 63.4 us
    psum x1 -> x0, waiting for transfers between devices: 29.6 us -> none  [per_device(): fock_ov = lax.psum(local_fock, 'pb') / (batch * lax.axis_size('pb'))]
    all_gather x0 -> x1, blocking collectives: none -> 9.29 us  [register_shelves_now(): z = jnp.sum(lax.all_gather(field_in, lane_axis), axis=0)]
  transfers between devices with their start and end apart: 3 -> 2, of which waited for: 3 -> 2; matrix products, arithmetic and copies ran while one was open for 5% -> 5% of each run, Pallas kernels for 0% -> 0%
where the time goes in v1:
time: 373 us; the launch traced here: 372 us
  waiting for transfers between devices  210 us (56%)
  blocking collectives  63.4 us (17%)
  matrix products  43.3 us (12%)
  local copies, waits for them, and re-layouts  33.9 us (9%)
  between operations  14.1 us (4%)
  starting transfers between devices  4.96 us (1%)
    all_to_all x1, waiting for transfers between devices, per_device(): lax.all_to_all(local_dressed, 'pq', split_axis=1, concat_axis=2, tiled=True)  136 us
    all_gather x1, waiting for transfers between devices, per_device(): lax.all_gather(lprime, 'pq', axis=1, tiled=True)  73.5 us
    all_gather x1, blocking collectives, per_device(): whole_amps = lax.all_gather(amplitudes, 'pq', axis=1, tiled=True)  34.5 us
    all_to_all x3, local copies, waits for them, and re-layouts, per_device(): lax.all_to_all(local_dressed, 'pq', split_axis=1, concat_axis=2, tiled=True)  24.4 us
    dot_general x1, matrix products, per_device(): jnp.einsum('qab,ib->qia', chol_vv, whole_amps, preferred_element_type=jnp...  19.8 us
    psum x1, blocking collectives, per_device(): coulomb = lax.psum(local_coulomb, 'pq')  19.7 us
    dot_general x1, matrix products, per_device(): jnp.einsum('qji,ja->qia', lax.all_gather(lprime, 'pq', axis=1, tiled=True...  10.7 us
    all_gather x1, blocking collectives, register_shelves_now(): z = jnp.sum(lax.all_gather(field_in, lane_axis), axis=0)  9.29 us
  transfers between devices with their start and end apart: 2, of which 2 were waited for; matrix products, arithmetic and copies ran while one was open for 5% of the time, Pallas kernels for 0%

profile of v1, /device:TPU:0, one launch (start us, length us, event | category | flops | bytes accessed | tf_op | source)
XLA Modules:
  0.0 372.0 jit_solution(1380634320363192755)
XLA Ops:
  7.2 0.0 all-gather.2.cloned.1.call-start
  7.2 34.5 %all_gather.12 = bf16[256,1792]{0,1:T(8,128)(2,1)S(1)} all-gather(bf16[256,224]{0,1:T(8,128)(2,1)} %param.9), channel_id=1, replica_groups=mesh['pb'=4,'pq'=8] {'pq'}, dimensions={1}, use_global_device_ids=true | all-gather | bytes 1032192 | tf_op jit(solution)/shard_map/all_gather | solution.py:15
  41.7 5.0 %add_convert_fusion = bf16[44,32,256]{2,1,0:T(8,128)(2,1)} fusion(bf16[44,32,256]{2,1,0:T(8,128)(2,1)} %param.7, bf16[44,32,1792]{2,1,0:T(8,128)(2,1)} %param.6, bf16[256,1792]{0,1:T(8,128)(2,1)S(1)} %all_gather.12), kind=kOutput, calls=%fused_computation.6 | convolution fusion | flops 1292926976 | bytes 7405568 | tf_op jit(solution)/shard_map/qjb,ib->qji/dot_general | solution.py:18
  46.6 0.0 all-gather.2.cloned.1.call-update
  46.6 0.0 copy-start
  46.7 19.8 %fusion.11 = f32[256,44,224]{0,2,1:T(8,128)} fusion(bf16[44,224,1792]{2,1,0:T(8,128)(2,1)} %param.5, bf16[256,1792]{0,1:T(8,128)(2,1)S(1)} %all_gather.12), kind=kOutput, calls=%fused_computation.10 | convolution fusion | flops 9042919424 | bytes 46333952 | tf_op jit(solution)/shard_map/qab,ib->qia/dot_general | solution.py:20
  66.4 73.5 %all-gather.2.cloned.1.call-done = bf16[44,256,256]{2,1,0:T(8,128)(2,1)} async-done(((bf16[44,32,256]{2,1,0:T(8,128)(2,1)}), bf16[44,256,256]{2,1,0:T(8,128)(2,1)}) %all-gather.2.cloned.1.call-update) | async-done | bytes 5767184 | tf_op jit(solution)/shard_map/all_gather | solution.py:24
  139.9 10.7 %fusion.1 = bf16[44,256,224]{1,2,0:T(8,128)(2,1)} fusion(f32[256,44,224]{0,2,1:T(8,128)} %fusion.11, bf16[44,256,224]{1,2,0:T(8,128)(2,1)} %param.8, bf16[44,256,256]{2,1,0:T(8,128)(2,1)} %all-gather.2.cloned.1.call-done, bf16[256,224]{0,1:T(8,128)(2,1)S(1)} %copy-done), kind=kOutput, calls=%fused_computation.3 | convolution fusion | flops 1301938176 | bytes 26066944 | tf_op jit(solution)/shard_map/qji,ja->qia/dot_general | solution.py:22
  150.6 8.7 %copy.14 = bf16[44,256,224]{2,0,1:T(8,128)(2,1)} copy(bf16[44,256,224]{1,2,0:T(8,128)(2,1)} %fusion.1) | data formatting | bytes 10092544 | tf_op jit(solution)/shard_map/convert_element_type | solution.py:28
  159.4 4.9 %all-to-all-start = ((bf16[44,256,224]{2,0,1:T(8,128)(2,1)}), bf16[44,256,224]{2,0,1:T(8,128)(2,1)}, u32[]{:S(2)}, u32[]{:S(2)}) async-start(bf16[44,256,224]{2,0,1:T(8,128)(2,1)} %copy.14), calls=%async_computation | async-start | bytes 12582912 | tf_op jit(solution)/shard_map/all_to_all | solution.py:29
  164.3 0.2 dynamic-slice_bitcast_fusion
  164.5 0.3 copy.19
  164.8 136.2 %all-to-all-done = bf16[44,256,224]{2,0,1:T(8,128)(2,1)} async-done(((bf16[44,256,224]{2,0,1:T(8,128)(2,1)}), bf16[44,256,224]{2,0,1:T(8,128)(2,1)}, u32[]{:S(2)}, u32[]{:S(2)}) %all-to-all-start) | async-done | bytes 5046304 | tf_op jit(solution)/shard_map/all_to_all | solution.py:29
  301.0 8.6 %copy.16 = bf16[44,32,8,224]{3,2,1,0:T(8,128)(2,1)} copy(bf16[44,32,8,224]{3,0,1,2:T(8,128)(2,1)} %bitcast.5) | data formatting | bytes 10092544 | tf_op jit(solution)/shard_map/all_to_all | solution.py:29
  309.6 11.0 %all_to_all.16 = bf16[44,32,1792]{2,1,0:T(8,128)(2,1)} reshape(bf16[44,32,8,224]{3,2,1,0:T(8,128)(2,1)} %copy.16) | data formatting | bytes 10092544 | tf_op jit(solution)/shard_map/all_to_all | solution.py:29
  320.5 7.9 %fusion.7 = f32[44]{0:T(128)S(1)} fusion(bf16[32,1792,1]{1,2,0:T(2,128)(2,1)S(1)} %copy.19, bf16[44,32,1792]{2,1,0:T(8,128)(2,1)} %all_to_all.16), kind=kOutput, calls=%fused_computation.8 | convolution fusion | flops 5046316 | bytes 5161136 | tf_op jit(solution)/shard_map/qia,ia->q/dot_general | solution.py:32
  328.4 19.7 %psum.7 = f32[44]{0:T(128)S(1)} all-reduce(f32[44]{0:T(128)S(1)} %fusion.7), channel_id=1, replica_groups=mesh['pb'=4,'pq'=8] {'pq'}, use_global_device_ids=true, to_apply=%region_0.0 | all-reduce | flops 44 | bytes 352 | tf_op jit(solution)/shard_map/psum | solution.py:35
  348.1 4.8 %copy.15 = bf16[44,256,224]{2,1,0:T(8,128)(2,1)S(1)} copy(bf16[44,256,224]{2,0,1:T(8,128)(2,1)} %all-to-all-done) | data formatting | bytes 10092544 | tf_op jit(solution)/shard_map/all_to_all | solution.py:29
  352.9 1.9 multiply_reduce_fusion
  354.8 0.2 copy.17
  354.9 0.1 all_gather.14
  355.1 9.3 %all_gather.15 = f32[4,32,1792]{2,1,0:T(8,128)S(1)} all-gather(f32[1,32,1792]{2,1,0:T(8,128)S(1)} %all_gather.14), channel_id=1, replica_groups=mesh['pb'=4,'pq'=8] {'pb'}, dimensions={0}, use_global_device_ids=true | all-gather | bytes 1146880 | tf_op jit(solution)/shard_map/all_gather | solution.py:8
  364.4 0.1 reduce_sum.19
  364.4 0.7 broadcast_multiply_fusion
  (1 shorter events, 0.0 us)
Async XLA Ops:
  7.2 132.8 %all-gather.2.cloned.1.call-start = ((), (), s32[]{:S(2)}) async-start(), calls=%async_computation.1 | async-start | bytes 6488064 | tf_op jit(solution)/shard_map/all_gather | solution.py:24
  46.6 93.3 %copy-start = (bf16[256,224]{0,1:T(8,128)(2,1)S(1)}, bf16[256,224]{0,1:T(8,128)(2,1)}, u32[]{:S(2)}) copy-start(bf16[256,224]{0,1:T(8,128)(2,1)} %param.9) | copy-start | bytes 344068
  159.4 141.6 %all-to-all-start = ((bf16[44,256,224]{2,0,1:T(8,128)(2,1)}), bf16[44,256,224]{2,0,1:T(8,128)(2,1)}, u32[]{:S(2)}, u32[]{:S(2)}) async-start(bf16[44,256,224]{2,0,1:T(8,128)(2,1)} %copy.14), calls=%async_computation | async-start | bytes 12582912 | tf_op jit(solution)/shard_map/all_to_all | solution.py:29
Sparse Core Ops, SparseCore 0:
  46.8 93.1 all-gather.1
